TPU v7x, 128 devices: a whole 4x4x4 slice. The times are simulated.
128 devices in a mesh: gx: 16 (over y, x), gy: 8 (over z, core).
Axes of the slice: x: 4, y: 4, z: 4, core: 2. Of those that a mesh axis runs over, the one named last changes fastest.
Arguments:
- basis: float32 [32, 256, 128, 256], P(None, 'gx', 'gy'), may hold values from -0.09375 to 0.09375
- reaction: float32 [256, 128, 256], P('gx', 'gy'), may hold values from 0.5 to 4
Outputs:
- extended: float32 [32, 256, 128, 256], P(None, 'gx', 'gy')
- coarse: float32 [128, 5, 32, 32], replicated
All inputs are finite; a program needn't handle non-finite values.
Results may differ from a plain program's by a relative error of at most 0.000071.
Values sent between devices are 32-bit elements; how exact they have to be, the bound alone decides.
No kernel may reach another device: no remote copies, remote signals or barrier semaphores. Data moves between devices by JAX's collectives and lax.ppermute only.
A program may use at most 128 MiB of HBM per device.

v0:
```python
import jax
import jax.numpy as jnp
from jax import lax
from jax.sharding import PartitionSpec as P

SWEEPS = 4


OMEGA = 0.8


def with_halo(shard, sides, width):
    edges = {}
    for axis, dim in sides:
        size, length = (lax.axis_size(axis), shard.shape[dim])
        up = [(i, (i + 1) % size) for i in range(size - 1)]
        last = lax.slice_in_dim(shard, length - width, length, axis=dim)
        first = lax.slice_in_dim(shard, 0, width, axis=dim)
        edges[dim] = (
            lax.ppermute(last, axis, up),
            lax.ppermute(first, axis, [(b, a) for a, b in up]),
        )
    done = []
    for _, dim in sides:
        low, high = edges[dim]
        around = [(width, width) if d in done else (0, 0) for d in range(shard.ndim)]
        shard = jnp.concatenate([jnp.pad(low, around), shard, jnp.pad(high, around)], axis=dim)
        done.append(dim)
    return shard


def stencil(field, coef):
    padded = jnp.pad(field, ((0, 0), (1, 1), (1, 1), (1, 1)))
    beside = padded[:, 2:, 1:-1, 1:-1] + padded[:, :-2, 1:-1, 1:-1]
    beside = beside + padded[:, 1:-1, 2:, 1:-1] + padded[:, 1:-1, :-2, 1:-1]
    beside = beside + padded[:, 1:-1, 1:-1, 2:] + padded[:, 1:-1, 1:-1, :-2]
    return (6.0 + coef) * field - beside


def couple(own, other):
    width = own.shape[0]
    return -jnp.dot(
        own.reshape(width, -1),
        other.reshape(width, -1).T,
        precision=lax.Precision.HIGHEST,
        preferred_element_type=jnp.float32,
    )


def on_device(basis, reaction):
    width, cx, cy, cz = basis.shape
    padded = with_halo(basis, (("gx", 1), ("gy", 2)), 1)
    left_face = padded[:, 0, 1:-1, :]
    right_face = padded[:, -1, 1:-1, :]
    lower_face = padded[:, 1:-1, 0, :]
    upper_face = padded[:, 1:-1, -1, :]
    xpos = lax.broadcasted_iota(jnp.int32, (cx, cy, cz), 0)
    ypos = lax.broadcasted_iota(jnp.int32, (cx, cy, cz), 1)
    inner = (xpos >= 1) & (xpos <= cx - 2) & (ypos >= 1) & (ypos <= cy - 2)
    phi = basis
    for sweep in range(SWEEPS):
        update = OMEGA * stencil(phi, reaction) / (6.0 + reaction)
        phi = phi - jnp.where(inner[None], update, jnp.float32(0.0))
    applied = stencil(phi, reaction)
    diag = jnp.dot(
        phi.reshape(width, -1),
        applied.reshape(width, -1).T,
        precision=lax.Precision.HIGHEST,
        preferred_element_type=jnp.float32,
    )
    blocks = jnp.stack(
        [
            diag,
            couple(basis[:, 0], left_face),
            couple(basis[:, -1], right_face),
            couple(basis[:, :, 0], lower_face),
            couple(basis[:, :, -1], upper_face),
        ]
    )
    coarse = lax.all_gather(blocks[None], ("gx", "gy"), axis=0, tiled=True)
    return (phi, coarse)


def solution(mesh):
    placed = (P(None, "gx", "gy", None), P("gx", "gy", None))
    return jax.shard_map(
        on_device,
        mesh=mesh,
        in_specs=placed,
        out_specs=(P(None, "gx", "gy", None), P()),
        check_vma=False,
    )
```

profile of v0, /device:TPU:1, one launch (start us, length us, event | category | flops | bytes accessed | tf_op | source)
XLA Modules:
  0.0 217.7 jit_solution(16846393999798236059)
XLA Ops:
  7.2 0.0 all-gather.3.cloned.1.call-start
  7.2 0.0 copy-start.1
  7.2 1.4 fusion.77
  8.7 1.1 copy.20
  9.8 4.9 %collective-permute-start = (f32[32,1,16,256]{3,0,2,1:T(8,128)}, f32[32,1,16,256]{3,0,2,1:T(8,128)}, u32[]{:S(2)}, u32[]{:S(2)}) collective-permute-start(f32[32,1,16,256]{3,0,2,1:T(8,128)} %copy.20), channel_id=1, source_target_pairs={{0,8},{8,16},{16,24},{24,32},{32,40},{40,48},{48,56},{56,64},{64,7... | collective-permute-start | bytes 1572872 | tf_op jit(solution)/shard_map/ppermute | solution.py:20
  14.6 1.1 copy.19
  15.8 1.3 collective-permute-start.1
  17.1 4.4 %fusion.76 = (f32[32,16,1,256]{3,2,1,0:T(1,128)S(1)}, f32[32,16,1,256]{3,2,1,0:T(1,128)S(1)}) fusion(f32[32,16,16,256]{3,2,1,0:T(8,128)} %param.2), kind=kLoop, calls=%fused_computation.110 | loop fusion | bytes 2097152 | tf_op jit(solution)/shard_map/slice | solution.py:76
  21.5 1.1 copy.22
  22.6 4.4 %collective-permute-start.2 = (f32[32,16,1,256]{3,0,1,2:T(8,128)}, f32[32,16,1,256]{3,0,1,2:T(8,128)}, u32[]{:S(2)}, u32[]{:S(2)}) collective-permute-start(f32[32,16,1,256]{3,0,1,2:T(8,128)} %copy.22), channel_id=1, source_target_pairs={{0,1},{1,2},{2,3},{3,4},{4,5},{5,6},{6,7},{8,9},{9,10},{10,11},{11... | collective-permute-start | bytes 1572872 | tf_op jit(solution)/shard_map/ppermute | solution.py:20
  27.0 1.1 copy.21
  28.1 2.1 collective-permute-start.3
  30.2 1.0 broadcast_add_fusion
  31.2 0.1 and_and_fusion
  31.3 0.0 copy-done.1
  31.3 9.6 %select_subtract_fusion.3 = f32[32,16,16,256]{3,2,1,0:T(8,128)} fusion(f32[32,16,16,256]{3,2,1,0:T(8,128)S(1)} %copy-done.1, f32[16,16,256]{2,1,0:T(8,128)S(1)} %broadcast_add_fusion, pred[16,16,256]{2,1,0:T(8,128)(4,1)S(1)} %and_and_fusion), kind=kLoop, calls=%fused_computation.74 | loop fusion | flops 23068672 | bytes 17104896 | tf_op jit(solution)/shard_map/sub | solution.py:63
  40.9 21.9 %select_subtract_fusion.2 = f32[32,16,16,256]{3,2,1,0:T(8,128)S(1)} fusion(f32[32,16,16,256]{3,2,1,0:T(8,128)} %select_subtract_fusion.3, f32[16,16,256]{2,1,0:T(8,128)S(1)} %broadcast_add_fusion, pred[16,16,256]{2,1,0:T(8,128)(4,1)S(1)} %and_and_fusion), kind=kLoop, calls=%fused_computation.73 | loop fusion | flops 23068672 | bytes 17104896 | tf_op jit(solution)/shard_map/sub | solution.py:63
  62.8 9.6 %select_subtract_fusion.1 = f32[32,16,16,256]{3,2,1,0:T(8,128)} fusion(f32[32,16,16,256]{3,2,1,0:T(8,128)S(1)} %select_subtract_fusion.2, f32[16,16,256]{2,1,0:T(8,128)S(1)} %broadcast_add_fusion, pred[16,16,256]{2,1,0:T(8,128)(4,1)S(1)} %and_and_fusion), kind=kLoop, calls=%fused_computation.72 | loop fusion | flops 23068672 | bytes 17104896 | tf_op jit(solution)/shard_map/sub | solution.py:63
  72.4 21.9 %select_subtract_fusion = f32[32,16,16,256]{3,2,1,0:T(8,128)S(1)} fusion(f32[32,16,16,256]{3,2,1,0:T(8,128)} %select_subtract_fusion.1, f32[16,16,256]{2,1,0:T(8,128)S(1)} %broadcast_add_fusion, pred[16,16,256]{2,1,0:T(8,128)(4,1)S(1)} %and_and_fusion), kind=kLoop, calls=%fused_computation.71 | loop fusion | flops 23068672 | bytes 17104896 | tf_op jit(solution)/shard_map/sub | solution.py:63
  94.3 0.0 copy-start
  94.3 9.3 %fusion.37 = f32[32,16,16,256]{3,2,1,0:T(8,128)} fusion(f32[32,16,16,256]{3,2,1,0:T(8,128)S(1)} %select_subtract_fusion, f32[16,16,256]{2,1,0:T(8,128)S(1)} %broadcast_add_fusion), kind=kLoop, calls=%fused_computation.67 | loop fusion | flops 14680064 | bytes 17039360 | tf_op jit(solution)/shard_map/sub | solution.py:37
  103.6 0.0 copy-done
  103.6 16.2 %fusion.58 = f32[5,32,32]{2,1,0:T(8,128)S(1)} fusion(f32[32,16,16,256]{3,2,1,0:T(8,128)} %fusion.37, f32[32,16,16,256]{3,2,1,0:T(8,128)S(1)} %select_subtract_fusion), kind=kOutput, calls=%fused_computation.92 | convolution fusion | flops 805306368 | bytes 16793600 | tf_op jit(solution)/shard_map/dot_general | solution.py:65
  119.8 0.0 collective-permute-done
  119.8 1.9 fusion.52
  121.7 0.0 collective-permute-done.1
  121.7 1.9 fusion.49
  123.6 0.0 collective-permute-done.2
  123.6 1.9 fusion.46
  125.5 0.0 collective-permute-done.3
  125.5 0.8 fusion.43
  126.3 0.0 copy-start.2
  126.3 0.6 copy-done.2
  127.0 0.0 all-gather.3.cloned.1.call-update
  127.0 74.6 %all-gather.3.cloned.1.call-done = f32[640,32,32]{2,1,0:T(8,128)} async-done(((f32[5,32,32]{2,1,0:T(8,128)}), f32[640,32,32]{2,1,0:T(8,128)}) %all-gather.3.cloned.1.call-update) | async-done | bytes 2621456 | tf_op jit(solution)/shard_map/all_gather | solution.py:80
  201.6 9.2 %copy.17 = f32[128,5,32,32]{0,3,2,1:T(8,128)} copy(f32[128,5,32,32]{3,2,1,0:T(8,128)} %bitcast.81) | data formatting | bytes 5242880
  (2 shorter events, 0.0 us)
Async XLA Ops:
  7.2 194.4 %all-gather.3.cloned.1.call-start = ((), (), s32[]{:S(2)}) async-start(), calls=%async_computation | async-start | bytes 10567680 | tf_op jit(solution)/shard_map/all_gather | solution.py:80
  7.2 24.1 %copy-start.1 = (f32[32,16,16,256]{3,2,1,0:T(8,128)S(1)}, f32[32,16,16,256]{3,2,1,0:T(8,128)}, u32[]{:S(2)}) copy-start(f32[32,16,16,256]{3,2,1,0:T(8,128)} %param.2) | copy-start | bytes 25165828
  9.8 110.1 %collective-permute-start = (f32[32,1,16,256]{3,0,2,1:T(8,128)}, f32[32,1,16,256]{3,0,2,1:T(8,128)}, u32[]{:S(2)}, u32[]{:S(2)}) collective-permute-start(f32[32,1,16,256]{3,0,2,1:T(8,128)} %copy.20), channel_id=1, source_target_pairs={{0,8},{8,16},{16,24},{24,32},{32,40},{40,48},{48,56},{56,64},{64,7... | collective-permute-start | bytes 1572872 | tf_op jit(solution)/shard_map/ppermute | solution.py:20
  15.8 105.9 %collective-permute-start.1 = (f32[32,1,16,256]{3,0,2,1:T(8,128)}, f32[32,1,16,256]{3,0,2,1:T(8,128)}, u32[]{:S(2)}, u32[]{:S(2)}) collective-permute-start(f32[32,1,16,256]{3,0,2,1:T(8,128)} %copy.19), channel_id=1, source_target_pairs={{8,0},{16,8},{24,16},{32,24},{40,32},{48,40},{56,48},{64,56},{72,6... | collective-permute-start | bytes 1572872 | tf_op jit(solution)/shard_map/ppermute | solution.py:21
  22.6 101.0 %collective-permute-start.2 = (f32[32,16,1,256]{3,0,1,2:T(8,128)}, f32[32,16,1,256]{3,0,1,2:T(8,128)}, u32[]{:S(2)}, u32[]{:S(2)}) collective-permute-start(f32[32,16,1,256]{3,0,1,2:T(8,128)} %copy.22), channel_id=1, source_target_pairs={{0,1},{1,2},{2,3},{3,4},{4,5},{5,6},{6,7},{8,9},{9,10},{10,11},{11... | collective-permute-start | bytes 1572872 | tf_op jit(solution)/shard_map/ppermute | solution.py:20
  28.1 97.4 %collective-permute-start.3 = (f32[32,16,1,256]{3,0,1,2:T(8,128)}, f32[32,16,1,256]{3,0,1,2:T(8,128)S(1)}, u32[]{:S(2)}, u32[]{:S(2)}) collective-permute-start(f32[32,16,1,256]{3,0,1,2:T(8,128)} %copy.21), channel_id=1, source_target_pairs={{1,0},{2,1},{3,2},{4,3},{5,4},{6,5},{7,6},{9,8},{10,9},{11,10},{12... | collective-permute-start | bytes 1572872 | tf_op jit(solution)/shard_map/ppermute | solution.py:21
  94.3 9.3 %copy-start = (f32[32,16,16,256]{3,2,1,0:T(8,128)}, f32[32,16,16,256]{3,2,1,0:T(8,128)S(1)}, u32[]{:S(2)}) copy-start(f32[32,16,16,256]{3,2,1,0:T(8,128)S(1)} %select_subtract_fusion) | copy-start | bytes 25165828
  126.3 0.6 copy-start.2
Sparse Core Ops, SparseCore 0:
  127.1 74.4 all-gather.2
where the time goes:
time: 218 us
  waiting for transfers between devices  74.6 us (34%)
  other arithmetic  73.3 us (34%)
  matrix products  22.7 us (10%)
  local copies, waits for them, and re-layouts  20.2 us (9%)
  between operations  14.2 us (7%)
  starting transfers between devices  12.7 us (6%)
    all_gather x1, waiting for transfers between devices, on_device(): coarse = lax.all_gather(blocks[None], ('gx', 'gy'), axis=0, tiled=True)  74.6 us
    sub x4, other arithmetic, on_device(): phi = phi - jnp.where(inner[None], update, jnp.float32(0.0))  63 us
    dot_general x1, matrix products, on_device(): jnp.dot(phi.reshape(width, -1), applied.reshape(width, -1).T, precision=l...  16.2 us
    unnamed x11, local copies, waits for them, and re-layouts  14.3 us
    sub x1, other arithmetic, stencil(): return (6.0 + coef) * field - beside  9.28 us
    ppermute x2, starting transfers between devices, with_halo(): lax.ppermute(last, axis, up)  9.26 us
    dot_general x4, matrix products, couple(): jnp.dot(own.reshape(width, -1), other.reshape(width, -1).T, precision=lax...  6.45 us
    slice x1, local copies, waits for them, and re-layouts, on_device(): basis[:, :, 0]  4.41 us
  transfers between devices with their start and end apart: 5, of which 1 were waited for; matrix products, arithmetic and copies ran while one was open for 47% of the time, Pallas kernels for 0%

commit v1 on v0

v1 whole, which is shorter than its diff:
```python
import functools

import jax
import jax.numpy as jnp
from jax import lax
from jax.experimental import pallas as pl
from jax.experimental.pallas import tpu as pltpu
from jax.sharding import Mesh, PartitionSpec as P

K = 32
ROWS = 512
PITCH = 516
FPITCH = 36
OMEGA = 0.8
SWEEPS = 4
F32 = jnp.float32
BF16 = jnp.bfloat16
ANY = pl.BlockSpec(memory_space=pl.ANY)
VM = pl.BlockSpec(memory_space=pltpu.VMEM)


def rows_of(block):
    n = block.shape[0]
    return block.reshape(n, 16, 2, 8, 2, 128).transpose(0, 1, 2, 4, 3, 5).reshape(n, ROWS, 128)


def block_of(rows):
    n = rows.shape[0]
    return rows.reshape(n, 16, 2, 2, 8, 128).transpose(0, 1, 2, 4, 3, 5).reshape(n, 16, 16, 256)


def row(x, y, half):
    return x * 32 + (y // 8) * 16 + half * 8 + y % 8


def split(pair):
    high = pair.astype(BF16)
    return high, (pair - high.astype(F32)).astype(BF16)


def fold(square):
    return jnp.concatenate([square[8 * c : 8 * c + 8] for c in range(4)], axis=1)


def gram(left, right):
    full = lax.dot_general(left, right, (((1,), (1,)), ((), ())), preferred_element_type=F32)
    return full


def combine(full):
    return (full[32:, 32:] + full[32:, :32]) + full[:32, 32:] + full[:32, :32]


def main_kernel(b_hbm, r_hbm, o_hbm, g_ref, own_ref, st, w1, w2, rbuf, dbuf, p_ref, q_ref, acc, sem_in, sem_out, sem_r):
    def load_copy(k):
        return pltpu.make_async_copy(b_hbm.at[k], st.at[pl.ds(k * PITCH, ROWS)], sem_in.at[k])

    def store_copy(k):
        return pltpu.make_async_copy(st.at[pl.ds(k * PITCH, ROWS)], o_hbm.at[k], sem_out.at[k])

    rcopy = pltpu.make_async_copy(r_hbm, rbuf, sem_r)
    rcopy.start()
    for k in range(K):
        load_copy(k).start()
    rcopy.wait()

    @pl.loop(0, ROWS // 64)
    def _(i):
        part = pl.ds(pl.multiple_of(i * 64, 64), 64)
        center = 6.0 + rbuf[part, :]
        dbuf[part, :] = OMEGA / center
        rbuf[part, :] = 0.5 * center

    lane = lax.broadcasted_iota(jnp.int32, (8, 128), 1)
    first = lane == 0
    last = lane == 127
    zero = jnp.zeros((8, 128), F32)

    def z_sum(a, b):
        ra, rb = pltpu.roll(a, 1, 1), pltpu.roll(b, 1, 1)
        la, lb = pltpu.roll(a, 127, 1), pltpu.roll(b, 127, 1)
        return (
            jnp.where(first, zero, ra) + jnp.where(last, lb, la),
            jnp.where(first, ra, rb) + jnp.where(last, zero, lb),
        )

    def sweep(load, store):
        prev = None
        for x in range(0, 15):
            here = [None] * 16
            nxt = [None] * 16
            w = [None] * 15
            for y in range(0, 15):
                w[y] = [None, None]
                for h in range(2):
                    if x == 0 and y == 14:
                        continue
                    up = load(x, y + 1, h)
                    w[y][h] = up + load(x + 1, y, h)
                    here[y + 1] = here[y + 1] or [None, None]
                    here[y + 1][h] = up
                if x >= 1 and y >= 1:
                    c = here[y]
                    zs = z_sum(c[0], c[1])
                    for h in range(2):
                        s = (w[y][h] + prev[y - 1][h]) + zs[h]
                        d = dbuf[pl.ds(row(x, y, h), 8, stride=0), :]
                        store(x, y, h, (1.0 - OMEGA) * c[h] + d * s)
            prev = w

    @pl.loop(0, 4)
    def _(g):
        base = g * (8 * PITCH)

        @pl.loop(0, 8)
        def _(k):
            load_copy(g * 8 + k).wait()

        def stage(x, y, h):
            return pl.ds(base + row(x, y, h), 8, stride=PITCH)

        def work(x, y, h):
            return pl.ds(((x * 16 + y) * 2 + h) * 8, 8)

        def from_stage(x, y, h):
            return st[stage(x, y, h), :]

        def to_stage(x, y, h, v):
            st[stage(x, y, h), :] = v

        def reader(ref):
            return lambda x, y, h: ref[work(x, y, h), :]

        def writer(ref):
            def put(x, y, h, v):
                ref[work(x, y, h), :] = v

            return put

        for i in range(1, 15):
            for x, y in ((0, i), (15, i), (i, 0), (i, 15)):
                for h in range(2):
                    v = from_stage(x, y, h)
                    w1[work(x, y, h), :] = v
                    w2[work(x, y, h), :] = v
        sweep(from_stage, writer(w1))
        sweep(reader(w1), writer(w2))
        sweep(reader(w2), writer(w1))
        sweep(reader(w1), to_stage)

        @pl.loop(0, 8)
        def _(k):
            store_copy(g * 8 + k).start()

    def stage_pair(x, y, h, pair):
        at = x * 32 + ((y // 8) * 16 + h * 8 + y % 8)
        return [st[pl.ds(at + (2 * pair + o) * (8 * PITCH), 8, stride=PITCH), :] for o in range(2)]

    def halves(x, with_next):
        slot = lax.rem(x, 2)
        for pair in range(2):
            for h in range(2):
                pass
            up = [stage_pair(x, 0, h, pair) for h in range(2)]
            for y in range(16):
                c = up
                if y < 15:
                    up = [stage_pair(x, y + 1, h, pair) for h in range(2)]
                ahead = [stage_pair(x + 1, y, h, pair) for h in range(2)] if with_next else None
                q = [[None, None], [None, None]]
                for o in range(2):
                    a, b = c[0][o], c[1][o]
                    la, lb = pltpu.roll(a, 127, 1), pltpu.roll(b, 127, 1)
                    right = [jnp.where(last, lb, la), jnp.where(last, zero, lb)]
                    for h in range(2):
                        n = right[h]
                        if y < 15:
                            n = n + up[h][o]
                        if with_next:
                            n = n + ahead[h][o]
                        d = rbuf[pl.ds(x * 32 + ((y // 8) * 16 + h * 8 + y % 8), 8, stride=0), :]
                        q[h][o] = d * c[h][o] - n
                for h in range(2):
                    lanes = pl.ds(y * 256 + h * 128, 128)
                    hi, lo = split(jnp.concatenate(c[h], axis=0))
                    p_ref[slot, pl.ds(16 * pair, 16), lanes] = hi
                    p_ref[slot, pl.ds(32 + 16 * pair, 16), lanes] = lo
                    hi, lo = split(jnp.concatenate(q[h], axis=0))
                    q_ref[slot, pl.ds(16 * pair, 16), lanes] = hi
                    q_ref[slot, pl.ds(32 + 16 * pair, 16), lanes] = lo

    acc[...] = jnp.zeros_like(acc)
    halves(0, True)
    own_ref[0] = p_ref[0]

    @pl.loop(1, 15)
    def _(x):
        halves(x, True)
        slot = lax.rem(x - 1, 2)
        acc[...] += gram(p_ref[slot], q_ref[slot])

    halves(15, False)
    acc[...] += gram(p_ref[0], q_ref[0])
    acc[...] += gram(p_ref[1], q_ref[1])
    full = combine(acc[...])
    g_ref[...] = fold(full + full.T)

    for x in range(16):
        for pair in range(2):
            for h in range(2):
                hi, lo = split(jnp.concatenate(stage_pair(x, 0, h, pair), axis=0))
                lanes = pl.ds(x * 256 + h * 128, 128)
                own_ref[1, pl.ds(16 * pair, 16), lanes] = hi
                own_ref[1, pl.ds(32 + 16 * pair, 16), lanes] = lo

    for k in range(K):
        store_copy(k).wait()


def faces_kernel(b_hbm, x_ref, y_ref, sem):
    copies = [
        pltpu.make_async_copy(b_hbm.at[:, :, 1, :, pl.ds(7, 1), :], y_ref, sem.at[0]),
        pltpu.make_async_copy(b_hbm.at[:, 15], x_ref, sem.at[1]),
    ]
    for copy in copies:
        copy.start()
    for copy in copies:
        copy.wait()


def couple_kernel(copies, fx_hbm, fy_hbm, own_ref, g_ref, o_ref, sx, sy, p_ref, sem):
    def copy(which, ref, scratch, k):
        return pltpu.make_async_copy(ref.at[k], scratch.at[pl.ds(k * FPITCH, 32)], sem.at[which, k])

    sides = ((fx_hbm, sx), (fy_hbm, sy))
    for which, (ref, scratch) in enumerate(sides):
        for k in range(K):
            copy(which, ref, scratch, k).start()
    blocks = [g_ref[...]]
    for which, (ref, scratch) in enumerate(sides):
        for k in range(K):
            copy(which, ref, scratch, k).wait()
        for at in range(16):
            for h in range(2):
                line = row(0, at, h) if which == 0 else at * 2 + h
                for pair in range(2):
                    two = [scratch[pl.ds((2 * pair + o) * 8 * FPITCH + line, 8, stride=FPITCH), :] for o in range(2)]
                    hi, lo = split(jnp.concatenate(two, axis=0))
                    lanes = pl.ds(at * 256 + h * 128, 128)
                    p_ref[which, pl.ds(16 * pair, 16), lanes] = hi
                    p_ref[which, pl.ds(32 + 16 * pair, 16), lanes] = lo
        blocks.append(fold(-combine(gram(own_ref[which], p_ref[which]))))
    payload = jnp.concatenate(blocks, axis=0)
    for i in range(copies):
        o_ref[i] = payload


def finish_kernel(a_hbm, b_hbm, o_ref, a, b, m, t, sem):
    core = lax.rem(lax.axis_index("gy"), 2)
    for i, (src, dst) in enumerate(((a_hbm, a), (b_hbm, b))):
        pltpu.make_async_copy(src, dst, sem.at[i]).start()
    for i, (src, dst) in enumerate(((a_hbm, a), (b_hbm, b))):
        pltpu.make_async_copy(src, dst, sem.at[i]).wait()
    for block in range(3):
        for q in range(8):
            v = block * 8 + q
            for i, ref in enumerate((a, b)):
                c = core if i == 0 else 1 - core
                for j in range(8):
                    m[pl.ds(16 * j + c, 8, stride=2), :] = ref[pl.ds(v + 24 * 8 * j, 8, stride=24), :]
            turned = m[...].T
            for c in range(4):
                i = 8 * c + q
                part = turned[32 * c : 32 * c + 32]
                if block == 0:
                    o_ref[0, i] = part
                else:
                    o_ref[2 * block - 1, i] = part
                    t[pl.ds(i * 33, 32), :] = part
        if block:
            shift = 120 if block == 1 else 127
            for j in range(32):
                for i in range(4):
                    col = t[pl.ds(8 * i * 33 + j, 8, stride=33), :]
                    o_ref[2 * block, j, pl.ds(8 * i, 8), :] = pltpu.roll(col, shift, 1)


def on_device(basis, reaction):
    shape = jax.ShapeDtypeStruct
    rows = rows_of(basis)
    up_x, up_y = pl.pallas_call(
        faces_kernel,
        name="faces",
        out_shape=(shape((K, 2, 2, 8, 128), F32), shape((K, 16, 2, 1, 128), F32)),
        in_specs=[ANY],
        out_specs=(VM, VM),
        scratch_shapes=[pltpu.SemaphoreType.DMA((2,))],
    )(rows.reshape(K, 16, 2, 2, 8, 128))
    face_x = lax.ppermute(up_x.reshape(K, 32, 128), "gx", [(i, i + 1) for i in range(15)])
    face_y = lax.ppermute(up_y.reshape(K, 32, 128), "gy", [(i, i + 1) for i in range(7)])
    out, diag, own = pl.pallas_call(
        main_kernel,
        name="extend",
        out_shape=(shape((K, ROWS, 128), F32), shape((8, 128), F32), shape((2, 64, 4096), BF16)),
        in_specs=[ANY, ANY],
        out_specs=(ANY, VM, VM),
        scratch_shapes=[
            pltpu.VMEM((K * PITCH, 128), F32),
            pltpu.VMEM((4096, 128), F32),
            pltpu.VMEM((4096, 128), F32),
            pltpu.VMEM((ROWS, 128), F32),
            pltpu.VMEM((ROWS, 128), F32),
            pltpu.VMEM((2, 64, 4096), BF16),
            pltpu.VMEM((2, 64, 4096), BF16),
            pltpu.VMEM((64, 64), F32),
            pltpu.SemaphoreType.DMA((K,)),
            pltpu.SemaphoreType.DMA((K,)),
            pltpu.SemaphoreType.DMA,
        ],
        cost_estimate=pl.CostEstimate(flops=500_000_000, bytes_accessed=17_000_000, transcendentals=0),
    )(rows, rows_of(reaction[None])[0])
    payload = pl.pallas_call(
        functools.partial(couple_kernel, 64),
        name="couple",
        out_shape=shape((64, 24, 128), F32),
        in_specs=[ANY, ANY, VM, VM],
        out_specs=VM,
        scratch_shapes=[
            pltpu.VMEM((K * FPITCH, 128), F32),
            pltpu.VMEM((K * FPITCH, 128), F32),
            pltpu.VMEM((2, 64, 4096), BF16),
            pltpu.SemaphoreType.DMA((2, K)),
        ],
    )(face_x, face_y, own, diag)
    return out, payload


def finish(mine, other):
    shape = jax.ShapeDtypeStruct
    return pl.pallas_call(
        finish_kernel,
        name="finish",
        out_shape=shape((5, 32, 32, 128), F32),
        in_specs=[ANY, ANY],
        out_specs=VM,
        scratch_shapes=[
            pltpu.VMEM((64 * 24, 128), F32),
            pltpu.VMEM((64 * 24, 128), F32),
            pltpu.VMEM((128, 128), F32),
            pltpu.VMEM((32 * 33 + 7, 128), F32),
            pltpu.SemaphoreType.DMA((2,)),
        ],
    )(mine.reshape(64 * 24, 128), other.reshape(64 * 24, 128))


def solution(mesh):
    gx, gy = mesh.shape["gx"], mesh.shape["gy"]
    fine = Mesh(mesh.devices.reshape(gx, gy // 2, 2), ("gx", "gz", "core"))

    def local(basis, reaction):
        return on_device(basis, reaction)

    def exchange(payload):
        mine = lax.all_to_all(payload, ("gx", "gz"), 0, 0, tiled=True)
        return mine, lax.ppermute(mine, "core", [(0, 1), (1, 0)])

    def run(basis, reaction):
        rows, payload = jax.shard_map(
            local,
            mesh=mesh,
            in_specs=(P(None, "gx", "gy", None), P("gx", "gy", None)),
            out_specs=(P(("gx", "gy")), P(("gx", "gy"))),
            check_vma=False,
        )(basis, reaction)
        mine, other = jax.shard_map(
            exchange,
            mesh=fine,
            in_specs=P(("gx", "gz", "core")),
            out_specs=P(("gx", "gz", "core")),
            check_vma=False,
        )(payload)

        def last(rows, mine, other):
            return block_of(rows), finish(mine, other).transpose(3, 0, 1, 2)

        return jax.shard_map(
            last,
            mesh=mesh,
            in_specs=P(("gx", "gy")),
            out_specs=(P(None, "gx", "gy", None), P()),
            check_vma=False,
        )(rows, mine, other)

    return run
```

time: 218 us -> 79.7 us (0.37)
  other arithmetic: 73.3 us -> 0 us
  waiting for transfers between devices: 74.6 us -> 1.92 us
  Pallas kernels: 0 us -> 39.8 us
  blocking collectives: 0 us -> 26.6 us
  matrix products: 22.7 us -> 0 us
  local copies, waits for them, and re-layouts: 20.2 us -> 1.88 us
  between operations: 14.2 us -> 0.7 us
  starting transfers between devices: 12.7 us -> 8.47 us
    all_gather x1 -> x0, waiting for transfers between devices: 74.6 us -> none  [on_device(): coarse = lax.all_gather(blocks[None], ('gx', 'gy'), axis=0, tiled=True)]
    sub x5 -> x0, other arithmetic: 72.2 us -> none  [the longest x4 63 us: on_device(): phi = phi - jnp.where(inner[None], update, jnp.float32(0.0))]
    pallas_call x0 -> x4, Pallas kernels: none -> 39.8 us  [the longest x1 28.7 us: on_device(): pl.pallas_call(main_kernel, name='extend', out_shape=(shape((K, ROWS, 128...]
    all_to_all x0 -> x1, blocking collectives: none -> 26.6 us  [exchange(): mine = lax.all_to_all(payload, ('gx', 'gz'), 0, 0, tiled=True)]
    dot_general x5 -> x0, matrix products: 22.7 us -> none  [the longest x1 16.2 us: on_device(): jnp.dot(phi.reshape(width, -1), applied.reshape(width, -1).T, precision=l...]
    unnamed x11 -> x8, local copies, waits for them, and re-layouts: 14.3 us -> 1.88 us
    slice x2 -> x0, local copies, waits for them, and re-layouts: 5.84 us -> none  [the longest x1 4.41 us: on_device(): basis[:, :, 0]]
    ppermute x4 -> x3, starting transfers between devices: 12.6 us -> 8.47 us  [the longest x1 4.92 us: on_device(): lax.ppermute(up_y.reshape(K, 32, 128), 'gy', [(i, i + 1) for i in range(7)])]
  transfers between devices with their start and end apart: 5 -> 3, of which waited for: 1 -> 1; matrix products, arithmetic and copies ran while one was open for 47% -> 0% of each run, Pallas kernels for 0% -> 36%
where the time goes in v1:
time: 79.7 us; the launch traced here: 79.3 us
  Pallas kernels  39.8 us (50%)
  blocking collectives  26.6 us (33%)
  starting transfers between devices  8.47 us (11%)
  waiting for transfers between devices  1.92 us (2%)
  local copies, waits for them, and re-layouts  1.88 us (2%)
    pallas_call x1, Pallas kernels, on_device(): pl.pallas_call(main_kernel, name='extend', out_shape=(shape((K, ROWS, 128...  28.7 us
    all_to_all x1, blocking collectives, exchange(): mine = lax.all_to_all(payload, ('gx', 'gz'), 0, 0, tiled=True)  26.6 us
    ppermute x1, starting transfers between devices, on_device(): lax.ppermute(up_y.reshape(K, 32, 128), 'gy', [(i, i + 1) for i in range(7)])  4.92 us
    pallas_call x1, Pallas kernels, on_device(): pl.pallas_call(functools.partial(couple_kernel, 64), name='couple', out_s...  4.87 us
    pallas_call x1, Pallas kernels, finish(): pl.pallas_call(finish_kernel, name='finish', out_shape=shape((5, 32, 32,...  4 us
    ppermute x1, starting transfers between devices, on_device(): lax.ppermute(up_x.reshape(K, 32, 128), 'gx', [(i, i + 1) for i in range(1...  3.15 us
    pallas_call x1, Pallas kernels, on_device(): pl.pallas_call(faces_kernel, name='faces', out_shape=(shape((K, 2, 2, 8,...  2.21 us
    ppermute x1, waiting for transfers between devices, exchange(): return (mine, lax.ppermute(mine, 'core', [(0, 1), (1, 0)]))  1.91 us
  transfers between devices with their start and end apart: 3, of which 1 were waited for; matrix products, arithmetic and copies ran while one was open for 0% of the time, Pallas kernels for 36%

profile of v1, /device:TPU:1, one launch (start us, length us, event | category | flops | bytes accessed | tf_op | source)
XLA Modules:
  0.0 79.3 jit_solution(10430741820332436007)
XLA Ops:
  0.6 2.2 %faces.1 = (f32[32,2,2,8,128]{4,3,2,1,0:T(8,128)}, f32[32,16,2,1,128]{4,3,2,1,0:T(1,128)}) custom-call(f32[32,16,2,2,8,128]{5,4,3,2,1,0:T(8,128)} %bitcast.20), custom_call_target="tpu_custom_call" | custom-call | tf_op jit(solution)/shard_map/faces/pallas_call | solution.py:291
  2.8 4.9 %collective-permute-start.1 = (f32[32,32,128]{2,1,0:T(8,128)}, f32[32,32,128]{2,1,0:T(8,128)S(1)}, u32[]{:S(2)}, u32[]{:S(2)}) collective-permute-start(f32[32,32,128]{2,1,0:T(8,128)} %bitcast.28), channel_id=1, source_target_pairs={{0,1},{1,2},{2,3},{3,4},{4,5},{5,6},{6,7},{8,9},{9,10},{10,11},{11... | collective-permute-start | bytes 1572872 | tf_op jit(solution)/shard_map/ppermute | solution.py:300
  7.8 3.1 %collective-permute-start = (f32[32,32,128]{2,1,0:T(8,128)}, f32[32,32,128]{2,1,0:T(8,128)S(1)}, u32[]{:S(2)}, u32[]{:S(2)}) collective-permute-start(f32[32,32,128]{2,1,0:T(8,128)} %bitcast.27), channel_id=1, source_target_pairs={{0,8},{8,16},{16,24},{24,32},{32,40},{40,48},{48,56},{56,64},{64,7... | collective-permute-start | bytes 1572872 | tf_op jit(solution)/shard_map/ppermute | solution.py:299
  10.9 28.7 %extend.1 = (f32[32,512,128]{2,1,0:T(8,128)}, f32[8,128]{1,0:T(8,128)}, bf16[2,64,4096]{2,1,0:T(8,128)(2,1)}) custom-call(f32[32,512,128]{2,1,0:T(8,128)} %bitcast.21, f32[512,128]{1,0:T(8,128)} %bitcast.25), custom_call_target="tpu_custom_call" | custom-call | flops 500000000 | bytes 17000000 | tf_op jit(solution)/shard_map/extend/pallas_call | solution.py:301
  39.6 0.0 collective-permute-done.1.fy_hbm
  39.6 0.0 copy-start.2
  39.7 0.0 collective-permute-done.fx_hbm
  39.7 0.0 copy-start.3
  39.7 0.8 copy-done.2
  40.5 0.2 copy-done.3
  40.7 4.9 %couple.1 = f32[64,24,128]{2,1,0:T(8,128)} custom-call(f32[32,32,128]{2,1,0:T(8,128)} %copy-done.3, f32[32,32,128]{2,1,0:T(8,128)} %copy-done.2, bf16[2,64,4096]{2,1,0:T(8,128)(2,1)} %get-tuple-element.14.own_ref, f32[8,128]{1,0:T(8,128)} %get-tuple-element.15.g_ref), custom_call_target="tpu_custom_call" | custom-call | tf_op jit(solution)/shard_map/couple/pallas_call | solution.py:322
  45.5 26.6 %all_to_all.5 = f32[64,24,128]{2,1,0:T(8,128)S(1)} all-to-all(f32[64,24,128]{2,1,0:T(8,128)} %couple.1), channel_id=1, replica_groups=mesh['gx'=16,'gz'=4,'core'=2] {'gx','gz'}, dimensions={0} | all-to-all | bytes 1572864 | tf_op jit(solution)/shard_map/all_to_all | solution.py:364
  72.1 0.0 copy-start
  72.1 0.4 collective-permute-start.2
  72.5 1.9 %collective-permute-done.2 = f32[64,24,128]{2,1,0:T(8,128)S(1)} collective-permute-done((f32[64,24,128]{2,1,0:T(8,128)S(1)}, f32[64,24,128]{2,1,0:T(8,128)S(1)}, u32[]{:S(2)}, u32[]{:S(2)}) %collective-permute-start.2) | collective-permute-done | bytes 786464 | tf_op jit(solution)/shard_map/ppermute | solution.py:365
  74.4 0.0 copy-start.1
  74.4 0.0 copy-done
  74.4 0.9 %copy-done.1 = f32[64,24,128]{2,1,0:T(8,128)} copy-done((f32[64,24,128]{2,1,0:T(8,128)}, f32[64,24,128]{2,1,0:T(8,128)S(1)}, u32[]{:S(2)}) %copy-start.1) | copy-done | bytes 786456
  75.3 4.0 %finish.1 = f32[5,32,32,128]{3,2,1,0:T(8,128)} custom-call(f32[1536,128]{1,0:T(8,128)} %bitcast.22, f32[1536,128]{1,0:T(8,128)} %bitcast.24), custom_call_target="tpu_custom_call" | custom-call | tf_op jit(solution)/shard_map/finish/pallas_call | solution.py:340
Async XLA Ops:
  2.8 36.8 %collective-permute-start.1 = (f32[32,32,128]{2,1,0:T(8,128)}, f32[32,32,128]{2,1,0:T(8,128)S(1)}, u32[]{:S(2)}, u32[]{:S(2)}) collective-permute-start(f32[32,32,128]{2,1,0:T(8,128)} %bitcast.28), channel_id=1, source_target_pairs={{0,1},{1,2},{2,3},{3,4},{4,5},{5,6},{6,7},{8,9},{9,10},{10,11},{11... | collective-permute-start | bytes 1572872 | tf_op jit(solution)/shard_map/ppermute | solution.py:300
  7.8 31.9 %collective-permute-start = (f32[32,32,128]{2,1,0:T(8,128)}, f32[32,32,128]{2,1,0:T(8,128)S(1)}, u32[]{:S(2)}, u32[]{:S(2)}) collective-permute-start(f32[32,32,128]{2,1,0:T(8,128)} %bitcast.27), channel_id=1, source_target_pairs={{0,8},{8,16},{16,24},{24,32},{32,40},{40,48},{48,56},{56,64},{64,7... | collective-permute-start | bytes 1572872 | tf_op jit(solution)/shard_map/ppermute | solution.py:299
  39.6 0.8 %copy-start.2 = (f32[32,32,128]{2,1,0:T(8,128)}, f32[32,32,128]{2,1,0:T(8,128)S(1)}, u32[]{:S(2)}) copy-start(f32[32,32,128]{2,1,0:T(8,128)S(1)} %collective-permute-done.1.fy_hbm) | copy-start | bytes 1572868
  39.7 1.0 %copy-start.3 = (f32[32,32,128]{2,1,0:T(8,128)}, f32[32,32,128]{2,1,0:T(8,128)S(1)}, u32[]{:S(2)}) copy-start(f32[32,32,128]{2,1,0:T(8,128)S(1)} %collective-permute-done.fx_hbm) | copy-start | bytes 1572868
  72.1 2.3 %copy-start = (f32[64,24,128]{2,1,0:T(8,128)}, f32[64,24,128]{2,1,0:T(8,128)S(1)}, u32[]{:S(2)}) copy-start(f32[64,24,128]{2,1,0:T(8,128)S(1)} %all_to_all.5) | copy-start | bytes 2359300
  72.1 2.3 %collective-permute-start.2 = (f32[64,24,128]{2,1,0:T(8,128)S(1)}, f32[64,24,128]{2,1,0:T(8,128)S(1)}, u32[]{:S(2)}, u32[]{:S(2)}) collective-permute-start(f32[64,24,128]{2,1,0:T(8,128)S(1)} %all_to_all.5), channel_id=1, source_target_pairs={{0,1},{1,0},{2,3},{3,2},{4,5},{5,4},{6,7},{7,6},{8,9},{9,8},{10,11... | collective-permute-start | bytes 2359304 | tf_op jit(solution)/shard_map/ppermute | solution.py:365
  74.4 0.9 %copy-start.1 = (f32[64,24,128]{2,1,0:T(8,128)}, f32[64,24,128]{2,1,0:T(8,128)S(1)}, u32[]{:S(2)}) copy-start(f32[64,24,128]{2,1,0:T(8,128)S(1)} %collective-permute-done.2) | copy-start | bytes 2359300

commit v2 on v1

v2 whole, which is shorter than its diff:
```python
import functools

import jax
import jax.numpy as jnp
from jax import lax
from jax.experimental import pallas as pl
from jax.experimental.pallas import tpu as pltpu
from jax.sharding import Mesh, PartitionSpec as P

K = 32
ROWS = 512
PITCH = 516
FPITCH = 36
OMEGA = 0.8
SWEEPS = 4
F32 = jnp.float32
BF16 = jnp.bfloat16
ANY = pl.BlockSpec(memory_space=pltpu.HBM)
VM = pl.BlockSpec(memory_space=pltpu.VMEM)


def rows_of(block):
    n = block.shape[0]
    return block.reshape(n, 16, 2, 8, 2, 128).transpose(0, 1, 2, 4, 3, 5).reshape(n, ROWS, 128)


def block_of(rows):
    n = rows.shape[0]
    return rows.reshape(n, 16, 2, 2, 8, 128).transpose(0, 1, 2, 4, 3, 5).reshape(n, 16, 16, 256)


def row(x, y, half):
    return x * 32 + (y // 8) * 16 + half * 8 + y % 8


def split(pair):
    high = pair.astype(BF16)
    return high, (pair - high.astype(F32)).astype(BF16)


def fold(square):
    return jnp.concatenate([square[8 * c : 8 * c + 8] for c in range(4)], axis=1)


def put(ref, line, pair, two):
    high, low = split(jnp.concatenate(two, axis=0))
    ref[line, pl.ds(16 * pair, 16), :] = high
    ref[line, pl.ds(32 + 16 * pair, 16), :] = low


def gram(left, right):
    left = jnp.concatenate([left[i] for i in range(32)], axis=1)
    right = jnp.concatenate([right[i] for i in range(32)], axis=1)
    return lax.dot_general(left, right, (((1,), (1,)), ((), ())), preferred_element_type=F32)


def combine(full):
    return (full[32:, 32:] + full[32:, :32]) + full[:32, 32:] + full[:32, :32]


def main_kernel(b_hbm, r_ref, o_hbm, g_ref, own_ref, st, w1, w2, rbuf, dbuf, pa, qa, pb, qb, acc, sem_in, sem_out):
    def load_copy(k):
        return pltpu.make_async_copy(b_hbm.at[k], st.at[pl.ds(k * PITCH, ROWS)], sem_in.at[k])

    def store_copy(k):
        return pltpu.make_async_copy(st.at[pl.ds(k * PITCH, ROWS)], o_hbm.at[k], sem_out.at[k])

    for k in range(K):
        load_copy(k).start()

    @pl.loop(0, ROWS // 64)
    def _(i):
        part = pl.ds(pl.multiple_of(i * 64, 64), 64)
        center = 6.0 + r_ref[part, :]
        dbuf[part, :] = OMEGA / center
        rbuf[part, :] = 0.5 * center

    lane = lax.broadcasted_iota(jnp.int32, (8, 128), 1)
    first = lane == 0
    last = lane == 127
    zero = jnp.zeros((8, 128), F32)

    def z_sum(a, b):
        ra, rb = pltpu.roll(a, 1, 1), pltpu.roll(b, 1, 1)
        la, lb = pltpu.roll(a, 127, 1), pltpu.roll(b, 127, 1)
        return (
            jnp.where(first, zero, ra) + jnp.where(last, lb, la),
            jnp.where(first, ra, rb) + jnp.where(last, zero, lb),
        )

    def sweep(load, store):
        starts = [(0, j) for j in range(13, -1, -1)] + [(i, 0) for i in range(1, 14)]
        for x, y in starts:
            before = None
            while x <= 14 and y <= 14:
                ahead = [load(x, y + 1, h) + load(x + 1, y, h) for h in range(2)]
                if before is not None:
                    c = [load(x, y, h) for h in range(2)]
                    beside = z_sum(c[0], c[1])
                    for h in range(2):
                        total = (ahead[h] + before[h]) + beside[h]
                        d = dbuf[pl.ds(row(x, y, h), 8, stride=0), :]
                        store(x, y, h, (1.0 - OMEGA) * c[h] + d * total)
                before = ahead
                x, y = x + 1, y + 1

    @pl.loop(0, 4)
    def _(g):
        base = g * (8 * PITCH)

        @pl.loop(0, 8)
        def _(k):
            load_copy(g * 8 + k).wait()

        def stage(x, y, h):
            return pl.ds(base + row(x, y, h), 8, stride=PITCH)

        def work(x, y, h):
            return pl.ds(((x * 16 + y) * 2 + h) * 8, 8)

        def from_stage(x, y, h):
            return st[stage(x, y, h), :]

        def to_stage(x, y, h, v):
            st[stage(x, y, h), :] = v

        def reader(ref):
            return lambda x, y, h: ref[work(x, y, h), :]

        def writer(ref):
            def put(x, y, h, v):
                ref[work(x, y, h), :] = v

            return put

        for i in range(1, 15):
            for x, y in ((0, i), (15, i), (i, 0), (i, 15)):
                for h in range(2):
                    v = from_stage(x, y, h)
                    w1[work(x, y, h), :] = v
                    w2[work(x, y, h), :] = v
        sweep(from_stage, writer(w1))
        sweep(reader(w1), writer(w2))
        sweep(reader(w2), writer(w1))
        sweep(reader(w1), to_stage)

        @pl.loop(0, 8)
        def _(k):
            store_copy(g * 8 + k).start()

    def stage_pair(x, y, h, pair):
        at = x * 32 + ((y // 8) * 16 + h * 8 + y % 8)
        return [st[pl.ds(at + (2 * pair + o) * (8 * PITCH), 8, stride=PITCH), :] for o in range(2)]

    def halves(x, p_ref, q_ref, with_next=True):
        for pair in range(2):
            up = [stage_pair(x, 0, h, pair) for h in range(2)]
            for y in range(16):
                c = up
                if y < 15:
                    up = [stage_pair(x, y + 1, h, pair) for h in range(2)]
                ahead = [stage_pair(x + 1, y, h, pair) for h in range(2)] if with_next else None
                q = [[None, None], [None, None]]
                for o in range(2):
                    a, b = c[0][o], c[1][o]
                    la, lb = pltpu.roll(a, 127, 1), pltpu.roll(b, 127, 1)
                    right = [jnp.where(last, lb, la), jnp.where(last, zero, lb)]
                    for h in range(2):
                        n = right[h]
                        if y < 15:
                            n = n + up[h][o]
                        if with_next:
                            n = n + ahead[h][o]
                        d = rbuf[pl.ds(x * 32 + ((y // 8) * 16 + h * 8 + y % 8), 8, stride=0), :]
                        q[h][o] = d * c[h][o] - n
                for h in range(2):
                    put(p_ref, 2 * y + h, pair, c[h])
                    put(q_ref, 2 * y + h, pair, q[h])

    halves(0, pa, qa)
    own_ref[0] = pa[...]
    acc[...] = jnp.zeros_like(acc)

    @pl.loop(0, 7)
    def _(i):
        first_gram = gram(pa, qa)
        halves(2 * i + 1, pb, qb)
        second_gram = gram(pb, qb)
        halves(2 * i + 2, pa, qa)
        acc[...] += first_gram + second_gram

    first_gram = gram(pa, qa)
    halves(15, pb, qb, False)
    acc[...] += first_gram + gram(pb, qb)
    full = combine(acc[...])
    g_ref[...] = fold(full + full.T)

    for x in range(16):
        for pair in range(2):
            for h in range(2):
                put(own_ref.at[1], 2 * x + h, pair, stage_pair(x, 0, h, pair))

    for k in range(K):
        store_copy(k).wait()


def faces_kernel(b_hbm, rows_hbm, x_ref, y_ref, sem, sem_x):
    copies = [pltpu.make_async_copy(b_hbm.at[:, :, 1, :, pl.ds(7, 1), :], y_ref.at[:, pl.ds(0, 16)], sem)]
    for k in range(K):
        part = x_ref.at[pl.ds(k * FPITCH, 32)]
        copies.append(pltpu.make_async_copy(rows_hbm.at[k, pl.ds(480, 32)], part, sem_x.at[k]))
    for copy in copies:
        copy.start()
    for copy in copies:
        copy.wait()


def couple_kernel(copies, fx_ref, fy_ref, own_ref, g_ref, o_ref, p_ref):
    blocks = [g_ref[...]]
    for which, face in enumerate((fx_ref, fy_ref)):
        for at in range(16):
            for h in range(2):
                line = row(0, at, h) if which == 0 else at * 2 + h
                for pair in range(2):
                    two = [face[pl.ds((2 * pair + o) * 8 * FPITCH + line, 8, stride=FPITCH), :] for o in range(2)]
                    put(p_ref.at[which], 2 * at + h, pair, two)
        blocks.append(fold(-combine(gram(own_ref.at[which], p_ref.at[which]))))
    payload = jnp.concatenate(blocks, axis=0)
    for i in range(copies):
        o_ref[i] = payload


def finish_kernel(a, b, o_hbm, o_ref, m, t, sem):
    core = lax.rem(lax.axis_index("gy"), 2)

    def leave(block):
        return pltpu.make_async_copy(o_ref.at[block], o_hbm.at[block], sem.at[block])

    for block in range(3):
        for q in range(8):
            v = block * 8 + q
            for i, ref in enumerate((a, b)):
                c = core if i == 0 else 1 - core
                for j in range(8):
                    m[pl.ds(16 * j + c, 8, stride=2), :] = ref[pl.ds(v + 24 * 8 * j, 8, stride=24), :]
            turned = m[...].T
            for c in range(4):
                i = 8 * c + q
                part = turned[32 * c : 32 * c + 32]
                if block == 0:
                    o_ref[0, i] = part
                else:
                    o_ref[2 * block - 1, i] = part
                    t[pl.ds(i * 33, 32), :] = part
        if block:
            shift = 120 if block == 1 else 127
            for j in range(32):
                for i in range(4):
                    col = t[pl.ds(8 * i * 33 + j, 8, stride=33), :]
                    o_ref[2 * block, j, pl.ds(8 * i, 8), :] = pltpu.roll(col, shift, 1)
            leave(2 * block - 1).start()
            leave(2 * block).start()
        else:
            leave(0).start()
    for block in range(5):
        leave(block).wait()


def extend_call(rows, reaction):
    shape = jax.ShapeDtypeStruct
    return pl.pallas_call(
        main_kernel,
        name="extend",
        compiler_params=pltpu.CompilerParams(vmem_limit_bytes=57 << 20),
        out_shape=(shape((K, ROWS, 128), F32), shape((8, 128), F32), shape((2, 32, 64, 128), BF16)),
        in_specs=[ANY, VM],
        out_specs=(ANY, VM, VM),
        scratch_shapes=[
            pltpu.VMEM((K * PITCH, 128), F32),
            pltpu.VMEM((4096, 128), F32),
            pltpu.VMEM((4096, 128), F32),
            pltpu.VMEM((ROWS, 128), F32),
            pltpu.VMEM((ROWS, 128), F32),
            pltpu.VMEM((32, 64, 128), BF16),
            pltpu.VMEM((32, 64, 128), BF16),
            pltpu.VMEM((32, 64, 128), BF16),
            pltpu.VMEM((32, 64, 128), BF16),
            pltpu.VMEM((64, 64), F32),
            pltpu.SemaphoreType.DMA((K,)),
            pltpu.SemaphoreType.DMA((K,)),
        ],
        cost_estimate=pl.CostEstimate(flops=500_000_000, bytes_accessed=17_000_000, transcendentals=0),
    )(rows, reaction)


def on_device(basis, reaction):
    shape = jax.ShapeDtypeStruct
    rows = rows_of(basis)
    up_x, up_y = pl.pallas_call(
        faces_kernel,
        name="faces",
        compiler_params=pltpu.CompilerParams(vmem_limit_bytes=54 << 20),
        out_shape=(shape((K * FPITCH, 128), F32), shape((K, FPITCH // 2, 2, 1, 128), F32)),
        in_specs=[ANY, ANY],
        out_specs=(VM, VM),
        scratch_shapes=[pltpu.SemaphoreType.DMA, pltpu.SemaphoreType.DMA((K,))],
    )(rows.reshape(K, 16, 2, 2, 8, 128), rows)
    face_x = lax.ppermute(up_x, "gx", [(i, i + 1) for i in range(15)])
    face_y = lax.ppermute(up_y.reshape(K * FPITCH, 128), "gy", [(i, i + 1) for i in range(7)])
    out, diag, own = extend_call(rows, rows_of(reaction[None])[0])
    payload = pl.pallas_call(
        functools.partial(couple_kernel, 64),
        name="couple",
        compiler_params=pltpu.CompilerParams(vmem_limit_bytes=12 << 20),
        out_shape=shape((64, 24, 128), F32),
        in_specs=[VM, VM, VM, VM],
        out_specs=VM,
        scratch_shapes=[pltpu.VMEM((2, 32, 64, 128), BF16)],
    )(face_x, face_y, own, diag)
    return out, payload


def finish(mine, other):
    shape = jax.ShapeDtypeStruct
    return pl.pallas_call(
        finish_kernel,
        name="finish",
        compiler_params=pltpu.CompilerParams(vmem_limit_bytes=12 << 20),
        out_shape=shape((5, 32, 32, 128), F32),
        in_specs=[VM, VM],
        out_specs=ANY,
        scratch_shapes=[
            pltpu.VMEM((5, 32, 32, 128), F32),
            pltpu.VMEM((128, 128), F32),
            pltpu.VMEM((32 * 33 + 7, 128), F32),
            pltpu.SemaphoreType.DMA((5,)),
        ],
    )(mine.reshape(64 * 24, 128), other.reshape(64 * 24, 128))


def solution(mesh):
    gx, gy = mesh.shape["gx"], mesh.shape["gy"]
    fine = Mesh(mesh.devices.reshape(gx, gy // 2, 2), ("gx", "gz", "core"))

    def local(basis, reaction):
        return on_device(basis, reaction)

    def exchange(payload):
        mine = lax.all_to_all(payload, ("gx", "gz"), 0, 0, tiled=True)
        return mine, lax.ppermute(mine, "core", [(0, 1), (1, 0)])

    def run(basis, reaction):
        rows, payload = jax.shard_map(
            local,
            mesh=mesh,
            in_specs=(P(None, "gx", "gy", None), P("gx", "gy", None)),
            out_specs=(P(("gx", "gy")), P(("gx", "gy"))),
            check_vma=False,
        )(basis, reaction)
        mine, other = jax.shard_map(
            exchange,
            mesh=fine,
            in_specs=P(("gx", "gz", "core")),
            out_specs=P(("gx", "gz", "core")),
            check_vma=False,
        )(payload)

        def last(rows, mine, other):
            return block_of(rows), finish(mine, other).transpose(3, 0, 1, 2)

        return jax.shard_map(
            last,
            mesh=mesh,
            in_specs=P(("gx", "gy")),
            out_specs=(P(None, "gx", "gy", None), P()),
            check_vma=False,
        )(rows, mine, other)

    return run
```

time: 79.7 us -> 68.7 us (0.86)
  Pallas kernels: 39.8 us -> 29 us
    pallas_call x4, Pallas kernels: 39.8 us -> 29 us  [the longest x1 23.5 us: extend_call(): pl.pallas_call(main_kernel, name='extend', compiler_params=pltpu.Compiler...]
    unnamed x8 -> x4, local copies, waits for them, and re-layouts: 1.88 us -> 1.9 us
  transfers between devices with their start and end apart: 3 -> 3, of which waited for: 1 -> 1; matrix products, arithmetic and copies ran while one was open for 0% -> 0% of each run, Pallas kernels for 36% -> 34%
where the time goes in v2:
time: 68.7 us; the launch traced here: 68.4 us
  Pallas kernels  29 us (42%)
  blocking collectives  26.4 us (38%)
  starting transfers between devices  8.47 us (12%)
  waiting for transfers between devices  1.92 us (3%)
  local copies, waits for them, and re-layouts  1.9 us (3%)
  between operations  0.7 us (1%)
    all_to_all x1, blocking collectives, exchange(): mine = lax.all_to_all(payload, ('gx', 'gz'), 0, 0, tiled=True)  26.4 us
    pallas_call x1, Pallas kernels, extend_call(): pl.pallas_call(main_kernel, name='extend', compiler_params=pltpu.Compiler...  23.5 us
    ppermute x1, starting transfers between devices, on_device(): lax.ppermute(up_y.reshape(K * FPITCH, 128), 'gy', [(i, i + 1) for i in ra...  4.92 us
    ppermute x1, starting transfers between devices, on_device(): face_x = lax.ppermute(up_x, 'gx', [(i, i + 1) for i in range(15)])  3.15 us
    pallas_call x1, Pallas kernels, on_device(): pl.pallas_call(faces_kernel, name='faces', compiler_params=pltpu.Compiler...  2.47 us
    pallas_call x1, Pallas kernels, finish(): pl.pallas_call(finish_kernel, name='finish', compiler_params=pltpu.Compil...  2.37 us
    ppermute x1, waiting for transfers between devices, exchange(): return (mine, lax.ppermute(mine, 'core', [(0, 1), (1, 0)]))  1.91 us
    unnamed x4, local copies, waits for them, and re-layouts  1.9 us
  transfers between devices with their start and end apart: 3, of which 1 were waited for; matrix products, arithmetic and copies ran while one was open for 0% of the time, Pallas kernels for 34%

profile of v2, /device:TPU:1, one launch (start us, length us, event | category | flops | bytes accessed | tf_op | source)
XLA Modules:
  0.0 68.4 jit_solution(8066954888426953780)
XLA Ops:
  0.6 2.5 %faces.1 = (f32[1152,128]{1,0:T(8,128)}, f32[32,18,2,1,128]{4,3,2,1,0:T(1,128)}) custom-call(f32[32,16,2,2,8,128]{5,4,3,2,1,0:T(8,128)} %bitcast.22, f32[32,512,128]{2,1,0:T(8,128)} %bitcast.21), custom_call_target="tpu_custom_call" | custom-call | tf_op jit(solution)/shard_map/faces/pallas_call | solution.py:299
  3.1 4.9 %collective-permute-start.1 = (f32[1152,128]{1,0:T(8,128)}, f32[1152,128]{1,0:T(8,128)S(1)}, u32[]{:S(2)}, u32[]{:S(2)}) collective-permute-start(f32[1152,128]{1,0:T(8,128)} %bitcast.27), channel_id=1, source_target_pairs={{0,1},{1,2},{2,3},{3,4},{4,5},{5,6},{6,7},{8,9},{9,10},{10,11},{11... | collective-permute-start | bytes 1769480 | tf_op jit(solution)/shard_map/ppermute | solution.py:309
  8.0 3.2 %collective-permute-start = (f32[1152,128]{1,0:T(8,128)}, f32[1152,128]{1,0:T(8,128)S(1)}, u32[]{:S(2)}, u32[]{:S(2)}) collective-permute-start(f32[1152,128]{1,0:T(8,128)} %get-tuple-element.12), channel_id=1, source_target_pairs={{0,8},{8,16},{16,24},{24,32},{32,40},{40,48},{48,56},{56,64},{64,7... | collective-permute-start | bytes 1769480 | tf_op jit(solution)/shard_map/ppermute | solution.py:308
  11.2 23.5 %extend.1 = (f32[32,512,128]{2,1,0:T(8,128)}, f32[8,128]{1,0:T(8,128)}, bf16[2,32,64,128]{3,2,1,0:T(8,128)(2,1)}) custom-call(f32[32,512,128]{2,1,0:T(8,128)} %bitcast.23, f32[512,128]{1,0:T(8,128)} %bitcast.25), custom_call_target="tpu_custom_call" | custom-call | flops 500000000 | bytes 17000000 | tf_op jit(solution)/shard_map/extend/pallas_call | solution.py:271
  34.7 0.0 collective-permute-done.1.fy_ref
  34.7 0.0 collective-permute-done.fx_ref
  34.7 0.0 copy-start
  34.7 1.2 %copy-done = bf16[2,32,64,128]{3,2,1,0:T(8,128)(2,1)S(1)} copy-done((bf16[2,32,64,128]{3,2,1,0:T(8,128)(2,1)S(1)}, bf16[2,32,64,128]{3,2,1,0:T(8,128)(2,1)}, u32[]{:S(2)}) %copy-start) | copy-done | bytes 1048600
  36.0 0.0 copy-start.1
  36.0 0.7 copy-done.1
  36.6 0.7 %couple.1 = f32[64,24,128]{2,1,0:T(8,128)S(1)} custom-call(f32[1152,128]{1,0:T(8,128)S(1)} %collective-permute-done.fx_ref, f32[1152,128]{1,0:T(8,128)S(1)} %collective-permute-done.1.fy_ref, bf16[2,32,64,128]{3,2,1,0:T(8,128)(2,1)S(1)} %copy-done, f32[8,128]{1,0:T(8,128)S(1)} %copy-done.1), custom_call_target="tpu_custom_call" | custom-call | tf_op jit(solution)/shard_map/couple/pallas_call | solution.py:311
  37.3 26.4 %all_to_all.5 = f32[64,24,128]{2,1,0:T(8,128)S(1)} all-to-all(f32[64,24,128]{2,1,0:T(8,128)S(1)} %couple.1), channel_id=1, replica_groups=mesh['gx'=16,'gz'=4,'core'=2] {'gx','gz'}, dimensions={0} | all-to-all | bytes 1572864 | tf_op jit(solution)/shard_map/all_to_all | solution.py:349
  63.7 0.4 collective-permute-start.2
  64.1 1.9 %collective-permute-done.2 = f32[64,24,128]{2,1,0:T(8,128)S(1)} collective-permute-done((f32[64,24,128]{2,1,0:T(8,128)S(1)}, f32[64,24,128]{2,1,0:T(8,128)S(1)}, u32[]{:S(2)}, u32[]{:S(2)}) %collective-permute-start.2) | collective-permute-done | bytes 786464 | tf_op jit(solution)/shard_map/ppermute | solution.py:350
  66.0 2.4 %finish.1 = f32[5,32,32,128]{3,2,1,0:T(8,128)} custom-call(f32[1536,128]{1,0:T(8,128)S(1)} %bitcast.19, f32[1536,128]{1,0:T(8,128)S(1)} %bitcast.20), custom_call_target="tpu_custom_call" | custom-call | tf_op jit(solution)/shard_map/finish/pallas_call | solution.py:325
Async XLA Ops:
  3.1 31.6 %collective-permute-start.1 = (f32[1152,128]{1,0:T(8,128)}, f32[1152,128]{1,0:T(8,128)S(1)}, u32[]{:S(2)}, u32[]{:S(2)}) collective-permute-start(f32[1152,128]{1,0:T(8,128)} %bitcast.27), channel_id=1, source_target_pairs={{0,1},{1,2},{2,3},{3,4},{4,5},{5,6},{6,7},{8,9},{9,10},{10,11},{11... | collective-permute-start | bytes 1769480 | tf_op jit(solution)/shard_map/ppermute | solution.py:309
  8.0 26.7 %collective-permute-start = (f32[1152,128]{1,0:T(8,128)}, f32[1152,128]{1,0:T(8,128)S(1)}, u32[]{:S(2)}, u32[]{:S(2)}) collective-permute-start(f32[1152,128]{1,0:T(8,128)} %get-tuple-element.12), channel_id=1, source_target_pairs={{0,8},{8,16},{16,24},{24,32},{32,40},{40,48},{48,56},{56,64},{64,7... | collective-permute-start | bytes 1769480 | tf_op jit(solution)/shard_map/ppermute | solution.py:308
  34.7 1.2 %copy-start = (bf16[2,32,64,128]{3,2,1,0:T(8,128)(2,1)S(1)}, bf16[2,32,64,128]{3,2,1,0:T(8,128)(2,1)}, u32[]{:S(2)}) copy-start(bf16[2,32,64,128]{3,2,1,0:T(8,128)(2,1)} %get-tuple-element.14.own_ref) | copy-start | bytes 3145732
  36.0 0.7 copy-start.1
  63.7 2.3 %collective-permute-start.2 = (f32[64,24,128]{2,1,0:T(8,128)S(1)}, f32[64,24,128]{2,1,0:T(8,128)S(1)}, u32[]{:S(2)}, u32[]{:S(2)}) collective-permute-start(f32[64,24,128]{2,1,0:T(8,128)S(1)} %all_to_all.5), channel_id=1, source_target_pairs={{0,1},{1,0},{2,3},{3,2},{4,5},{5,4},{6,7},{7,6},{8,9},{9,8},{10,11... | collective-permute-start | bytes 2359304 | tf_op jit(solution)/shard_map/ppermute | solution.py:350

commit v3 on v2

--- a/solution.py
+++ b/solution.py
@@ -19,6 +19,12 @@
 VM = pl.BlockSpec(memory_space=pltpu.VMEM)
 
 
+STARTS = [(0, j) for j in range(13, -1, -1)] + [(i, 0) for i in range(1, 14)]
+ROTATED_STARTS = [p for p in STARTS if abs(p[0] - p[1]) < 5]
+LINED_STARTS = [p for p in STARTS if p not in ROTATED_STARTS]
+LINED = [(x + i, y + i) for x, y in LINED_STARTS for i in range(1, 15 - max(x, y))]
+
+
 def rows_of(block):
     n = block.shape[0]
     return block.reshape(n, 16, 2, 8, 2, 128).transpose(0, 1, 2, 4, 3, 5).reshape(n, ROWS, 128)
@@ -58,20 +64,29 @@
     return (full[32:, 32:] + full[32:, :32]) + full[:32, 32:] + full[:32, :32]
 
 
-def main_kernel(b_hbm, r_ref, o_hbm, g_ref, own_ref, st, w1, w2, rbuf, dbuf, pa, qa, pb, qb, acc, sem_in, sem_out):
+def main_kernel(b_hbm, r_hbm, o_hbm, g_ref, own_hbm, own_ref, st, w1, w2, rbuf, dbuf, pa, qa, pb, qb, acc, z_in, z_out, tri, sem_in, sem_out, sem_r, sem_own):
     def load_copy(k):
         return pltpu.make_async_copy(b_hbm.at[k], st.at[pl.ds(k * PITCH, ROWS)], sem_in.at[k])
 
     def store_copy(k):
         return pltpu.make_async_copy(st.at[pl.ds(k * PITCH, ROWS)], o_hbm.at[k], sem_out.at[k])
 
+    reaction = pltpu.make_async_copy(r_hbm, rbuf, sem_r)
+    reaction.start()
     for k in range(K):
         load_copy(k).start()
+
+    apart = lax.broadcasted_iota(jnp.int32, (256, 256), 0) - lax.broadcasted_iota(jnp.int32, (256, 256), 1)
+    band = jnp.where(jnp.abs(apart) == 1, 1.0, 0.0).astype(BF16)
+    tri[pl.ds(0, 256), :] = band
+    tri[pl.ds(256, 256), :] = band
+
+    reaction.wait()
 
     @pl.loop(0, ROWS // 64)
     def _(i):
         part = pl.ds(pl.multiple_of(i * 64, 64), 64)
-        center = 6.0 + r_ref[part, :]
+        center = 6.0 + rbuf[part, :]
         dbuf[part, :] = OMEGA / center
         rbuf[part, :] = 0.5 * center
 
@@ -89,14 +104,27 @@
         )
 
     def sweep(load, store):
-        starts = [(0, j) for j in range(13, -1, -1)] + [(i, 0) for i in range(1, 14)]
-        for x, y in starts:
+        for j in range(0, len(LINED), 2):
+            for h in range(2):
+                high, low = split(jnp.concatenate([load(*LINED[j], h), load(*LINED[j + 1], h)], axis=0))
+                z_in[h, pl.ds(8 * j, 16), :] = high
+                z_in[2 + h, pl.ds(8 * j, 16), :] = low
+        parts = jnp.concatenate([z_in[i] for i in range(4)], axis=1)
+        sums = lax.dot_general(parts, tri[...], (((1,), (0,)), ((), ())), preferred_element_type=F32)
+        for h in range(2):
+            z_out[h] = sums[:, 128 * h : 128 * h + 128]
+        for x, y in ROTATED_STARTS + LINED_STARTS:
+            lined = (x, y) in LINED_STARTS
             before = None
             while x <= 14 and y <= 14:
                 ahead = [load(x, y + 1, h) + load(x + 1, y, h) for h in range(2)]
                 if before is not None:
                     c = [load(x, y, h) for h in range(2)]
-                    beside = z_sum(c[0], c[1])
+                    if lined:
+                        at = pl.ds(8 * LINED.index((x, y)), 8)
+                        beside = [z_out[h, at, :] for h in range(2)]
+                    else:
+                        beside = z_sum(c[0], c[1])
                     for h in range(2):
                         total = (ahead[h] + before[h]) + beside[h]
                         d = dbuf[pl.ds(row(x, y, h), 8, stride=0), :]
@@ -179,6 +207,9 @@
 
     halves(0, pa, qa)
     own_ref[0] = pa[...]
+    leave_x = pltpu.make_async_copy(own_ref.at[0], own_hbm.at[0], sem_own.at[0])
+    leave_y = pltpu.make_async_copy(own_ref.at[1], own_hbm.at[1], sem_own.at[1])
+    leave_x.start()
     acc[...] = jnp.zeros_like(acc)
 
     @pl.loop(0, 7)
@@ -191,15 +222,17 @@
 
     first_gram = gram(pa, qa)
     halves(15, pb, qb, False)
-    acc[...] += first_gram + gram(pb, qb)
-    full = combine(acc[...])
-    g_ref[...] = fold(full + full.T)
-
     for x in range(16):
         for pair in range(2):
             for h in range(2):
                 put(own_ref.at[1], 2 * x + h, pair, stage_pair(x, 0, h, pair))
-
+    leave_y.start()
+    acc[...] += first_gram + gram(pb, qb)
+    full = combine(acc[...])
+    g_ref[...] = fold(full + full.T)
+
+    leave_x.wait()
+    leave_y.wait()
     for k in range(K):
         store_copy(k).wait()
 
@@ -215,8 +248,13 @@
         copy.wait()
 
 
-def couple_kernel(copies, fx_ref, fy_ref, own_ref, g_ref, o_ref, p_ref):
-    blocks = [g_ref[...]]
+def couple_kernel(copies, fx_ref, fy_ref, own_hbm, g_hbm, o_ref, p_ref, own_ref, g_ref, sem):
+    get = [
+        pltpu.make_async_copy(g_hbm, g_ref, sem.at[0]),
+        pltpu.make_async_copy(own_hbm, own_ref, sem.at[1]),
+    ]
+    for copy in get:
+        copy.start()
     for which, face in enumerate((fx_ref, fy_ref)):
         for at in range(16):
             for h in range(2):
@@ -224,6 +262,10 @@
                 for pair in range(2):
                     two = [face[pl.ds((2 * pair + o) * 8 * FPITCH + line, 8, stride=FPITCH), :] for o in range(2)]
                     put(p_ref.at[which], 2 * at + h, pair, two)
+    for copy in get:
+        copy.wait()
+    blocks = [g_ref[...]]
+    for which in range(2):
         blocks.append(fold(-combine(gram(own_ref.at[which], p_ref.at[which]))))
     payload = jnp.concatenate(blocks, axis=0)
     for i in range(copies):
@@ -271,11 +313,12 @@
     return pl.pallas_call(
         main_kernel,
         name="extend",
-        compiler_params=pltpu.CompilerParams(vmem_limit_bytes=57 << 20),
+        compiler_params=pltpu.CompilerParams(vmem_limit_bytes=46 << 20),
         out_shape=(shape((K, ROWS, 128), F32), shape((8, 128), F32), shape((2, 32, 64, 128), BF16)),
-        in_specs=[ANY, VM],
-        out_specs=(ANY, VM, VM),
+        in_specs=[ANY, ANY],
+        out_specs=(ANY, VM, ANY),
         scratch_shapes=[
+            pltpu.VMEM((2, 32, 64, 128), BF16),
             pltpu.VMEM((K * PITCH, 128), F32),
             pltpu.VMEM((4096, 128), F32),
             pltpu.VMEM((4096, 128), F32),
@@ -286,8 +329,13 @@
             pltpu.VMEM((32, 64, 128), BF16),
             pltpu.VMEM((32, 64, 128), BF16),
             pltpu.VMEM((64, 64), F32),
+            pltpu.VMEM((4, 8 * len(LINED), 128), BF16),
+            pltpu.VMEM((2, 8 * len(LINED), 128), F32),
+            pltpu.VMEM((512, 256), BF16),
             pltpu.SemaphoreType.DMA((K,)),
             pltpu.SemaphoreType.DMA((K,)),
+            pltpu.SemaphoreType.DMA,
+            pltpu.SemaphoreType.DMA((2,)),
         ],
         cost_estimate=pl.CostEstimate(flops=500_000_000, bytes_accessed=17_000_000, transcendentals=0),
     )(rows, reaction)
@@ -313,9 +361,14 @@
         name="couple",
         compiler_params=pltpu.CompilerParams(vmem_limit_bytes=12 << 20),
         out_shape=shape((64, 24, 128), F32),
-        in_specs=[VM, VM, VM, VM],
+        in_specs=[VM, VM, ANY, ANY],
         out_specs=VM,
-        scratch_shapes=[pltpu.VMEM((2, 32, 64, 128), BF16)],
+        scratch_shapes=[
+            pltpu.VMEM((2, 32, 64, 128), BF16),
+            pltpu.VMEM((2, 32, 64, 128), BF16),
+            pltpu.VMEM((8, 128), F32),
+            pltpu.SemaphoreType.DMA((2,)),
+        ],
     )(face_x, face_y, own, diag)
     return out, payload
 

time: 68.7 us -> 62 us (0.902)
  Pallas kernels: 29 us -> 24.3 us
  local copies, waits for them, and re-layouts: 1.9 us -> 0.01 us
    pallas_call x1, Pallas kernels: 23.5 us -> 18.6 us  [extend_call(): pl.pallas_call(main_kernel, name='extend', compiler_params=pltpu.Compiler...]
    unnamed x4 -> x2, local copies, waits for them, and re-layouts: 1.9 us -> 0.01 us
  transfers between devices with their start and end apart: 3 -> 3, of which waited for: 1 -> 1; matrix products, arithmetic and copies ran while one was open for 0% -> 0% of each run, Pallas kernels for 34% -> 30%
where the time goes in v3:
time: 62 us; the launch traced here: 61.8 us
  blocking collectives  26.4 us (43%)
  Pallas kernels  24.3 us (39%)
  starting transfers between devices  8.47 us (14%)
  waiting for transfers between devices  1.92 us (3%)
  between operations  0.7 us (1%)
    all_to_all x1, blocking collectives, exchange(): mine = lax.all_to_all(payload, ('gx', 'gz'), 0, 0, tiled=True)  26.4 us
    pallas_call x1, Pallas kernels, extend_call(): pl.pallas_call(main_kernel, name='extend', compiler_params=pltpu.Compiler...  18.6 us
    ppermute x1, starting transfers between devices, on_device(): lax.ppermute(up_y.reshape(K * FPITCH, 128), 'gy', [(i, i + 1) for i in ra...  4.92 us
    ppermute x1, starting transfers between devices, on_device(): face_x = lax.ppermute(up_x, 'gx', [(i, i + 1) for i in range(15)])  3.15 us
    pallas_call x1, Pallas kernels, on_device(): pl.pallas_call(faces_kernel, name='faces', compiler_params=pltpu.Compiler...  2.5 us
    pallas_call x1, Pallas kernels, finish(): pl.pallas_call(finish_kernel, name='finish', compiler_params=pltpu.Compil...  2.37 us
    ppermute x1, waiting for transfers between devices, exchange(): return (mine, lax.ppermute(mine, 'core', [(0, 1), (1, 0)]))  1.91 us
  transfers between devices with their start and end apart: 3, of which 1 were waited for; matrix products, arithmetic and copies ran while one was open for 0% of the time, Pallas kernels for 30%

profile of v3, /device:TPU:1, one launch (start us, length us, event | category | flops | bytes accessed | tf_op | source)
XLA Modules:
  0.0 61.8 jit_solution(10256904046190930363)
XLA Ops:
  0.6 0.0 copy-start
  0.6 2.5 %faces.1 = (f32[1152,128]{1,0:T(8,128)}, f32[32,18,2,1,128]{4,3,2,1,0:T(1,128)}) custom-call(f32[32,16,2,2,8,128]{5,4,3,2,1,0:T(8,128)} %bitcast.23, f32[32,512,128]{2,1,0:T(8,128)} %bitcast.22), custom_call_target="tpu_custom_call" | custom-call | tf_op jit(solution)/shard_map/faces/pallas_call | solution.py:347
  3.1 4.9 %collective-permute-start.1 = (f32[1152,128]{1,0:T(8,128)}, f32[1152,128]{1,0:T(8,128)S(1)}, u32[]{:S(2)}, u32[]{:S(2)}) collective-permute-start(f32[1152,128]{1,0:T(8,128)} %bitcast.27), channel_id=1, source_target_pairs={{0,1},{1,2},{2,3},{3,4},{4,5},{5,6},{6,7},{8,9},{9,10},{10,11},{11... | collective-permute-start | bytes 1769480 | tf_op jit(solution)/shard_map/ppermute | solution.py:357
  8.1 3.2 %collective-permute-start = (f32[1152,128]{1,0:T(8,128)}, f32[1152,128]{1,0:T(8,128)S(1)}, u32[]{:S(2)}, u32[]{:S(2)}) collective-permute-start(f32[1152,128]{1,0:T(8,128)} %get-tuple-element.12), channel_id=1, source_target_pairs={{0,8},{8,16},{16,24},{24,32},{32,40},{40,48},{48,56},{56,64},{64,7... | collective-permute-start | bytes 1769480 | tf_op jit(solution)/shard_map/ppermute | solution.py:356
  11.2 0.0 copy-done
  11.2 18.6 %extend.1 = (f32[32,512,128]{2,1,0:T(8,128)}, f32[8,128]{1,0:T(8,128)S(1)}, bf16[2,32,64,128]{3,2,1,0:T(8,128)(2,1)S(1)}) custom-call(f32[32,512,128]{2,1,0:T(8,128)} %bitcast.24, f32[512,128]{1,0:T(8,128)S(1)} %bitcast.21), custom_call_target="tpu_custom_call" | custom-call | flops 500000000 | bytes 17000000 | tf_op jit(solution)/shard_map/extend/pallas_call | solution.py:313
  29.9 0.0 collective-permute-done.1.fy_ref
  29.9 0.0 collective-permute-done.fx_ref
  29.9 0.8 %couple.1 = f32[64,24,128]{2,1,0:T(8,128)S(1)} custom-call(f32[1152,128]{1,0:T(8,128)S(1)} %collective-permute-done.fx_ref, f32[1152,128]{1,0:T(8,128)S(1)} %collective-permute-done.1.fy_ref, bf16[2,32,64,128]{3,2,1,0:T(8,128)(2,1)S(1)} %get-tuple-element.14.own_hbm, f32[8,128]{1,0:T(8,128)S(1)} %get-tuple-element.15.g_hbm), custom_call_target="tpu_custom_call" | custom-call | tf_op jit(solution)/shard_map/couple/pallas_call | solution.py:359
  30.7 26.4 %all_to_all.5 = f32[64,24,128]{2,1,0:T(8,128)S(1)} all-to-all(f32[64,24,128]{2,1,0:T(8,128)S(1)} %couple.1), channel_id=1, replica_groups=mesh['gx'=16,'gz'=4,'core'=2] {'gx','gz'}, dimensions={0} | all-to-all | bytes 1572864 | tf_op jit(solution)/shard_map/all_to_all | solution.py:402
  57.1 0.4 collective-permute-start.2
  57.5 1.9 %collective-permute-done.2 = f32[64,24,128]{2,1,0:T(8,128)S(1)} collective-permute-done((f32[64,24,128]{2,1,0:T(8,128)S(1)}, f32[64,24,128]{2,1,0:T(8,128)S(1)}, u32[]{:S(2)}, u32[]{:S(2)}) %collective-permute-start.2) | collective-permute-done | bytes 786464 | tf_op jit(solution)/shard_map/ppermute | solution.py:403
  59.4 2.4 %finish.1 = f32[5,32,32,128]{3,2,1,0:T(8,128)} custom-call(f32[1536,128]{1,0:T(8,128)S(1)} %bitcast.19, f32[1536,128]{1,0:T(8,128)S(1)} %bitcast.20), custom_call_target="tpu_custom_call" | custom-call | tf_op jit(solution)/shard_map/finish/pallas_call | solution.py:378
Async XLA Ops:
  0.6 10.6 %copy-start = (f32[16,16,256]{2,1,0:T(8,128)S(1)}, f32[16,16,256]{2,1,0:T(8,128)}, u32[]{:S(2)}) copy-start(f32[16,16,256]{2,1,0:T(8,128)} %param.7) | copy-start | bytes 786436
  3.1 26.7 %collective-permute-start.1 = (f32[1152,128]{1,0:T(8,128)}, f32[1152,128]{1,0:T(8,128)S(1)}, u32[]{:S(2)}, u32[]{:S(2)}) collective-permute-start(f32[1152,128]{1,0:T(8,128)} %bitcast.27), channel_id=1, source_target_pairs={{0,1},{1,2},{2,3},{3,4},{4,5},{5,6},{6,7},{8,9},{9,10},{10,11},{11... | collective-permute-start | bytes 1769480 | tf_op jit(solution)/shard_map/ppermute | solution.py:357
  8.1 21.8 %collective-permute-start = (f32[1152,128]{1,0:T(8,128)}, f32[1152,128]{1,0:T(8,128)S(1)}, u32[]{:S(2)}, u32[]{:S(2)}) collective-permute-start(f32[1152,128]{1,0:T(8,128)} %get-tuple-element.12), channel_id=1, source_target_pairs={{0,8},{8,16},{16,24},{24,32},{32,40},{40,48},{48,56},{56,64},{64,7... | collective-permute-start | bytes 1769480 | tf_op jit(solution)/shard_map/ppermute | solution.py:356
  57.1 2.3 %collective-permute-start.2 = (f32[64,24,128]{2,1,0:T(8,128)S(1)}, f32[64,24,128]{2,1,0:T(8,128)S(1)}, u32[]{:S(2)}, u32[]{:S(2)}) collective-permute-start(f32[64,24,128]{2,1,0:T(8,128)S(1)} %all_to_all.5), channel_id=1, source_target_pairs={{0,1},{1,0},{2,3},{3,2},{4,5},{5,4},{6,7},{7,6},{8,9},{9,8},{10,11... | collective-permute-start | bytes 2359304 | tf_op jit(solution)/shard_map/ppermute | solution.py:403
